TPU v7x, 32 devices: a whole 2x2x4 slice. The times are simulated.
32 devices in a mesh: gx: 4 (over y, x), gy: 4 (over z), gz: 2 (over core).
Axes of the slice: x: 2, y: 2, z: 4, core: 2. Of those that a mesh axis runs over, the one named last changes fastest.
Arguments:
- element_load: float32 [36, 36, 18, 128], P('gx', 'gy', 'gz'), may hold values from -90 to 90
- local_matrix: float32 [4, 4, 2, 729, 729], P('gx', 'gy', 'gz'), may hold values from -10 to 61, as said below
- dirichlet_inverse: float32 [4, 4, 2, 343, 343], P('gx', 'gy', 'gz'), as said below
- neumann_inverse: float32 [4, 4, 2, 729, 729], P('gx', 'gy', 'gz'), as said below
- coarse_basis: float32 [4, 4, 2, 20, 729], P('gx', 'gy', 'gz'), as said below
Outputs:
- solution: float32 [36, 36, 18, 128], P('gx', 'gy', 'gz')
- residual: float32 [36, 36, 18, 128], P('gx', 'gy', 'gz')
Inputs may be any that keep to these rules, and one draw needn't show every extreme that they name: `local_matrix`: block (a, b, c) is the symmetric positive definite stiffness matrix of subdomain (a, b, c) in the node order of the steps: cellwise conductivities on the couplings of neighbouring nodes plus a lumped reaction term. `dirichlet_inverse`: block (a, b, c) is the inverse, computed in float32, of local_matrix's block restricted to the inner nodes. `neumann_inverse`: block (a, b, c) is the node-by-node block of the inverse, computed in float32, of the saddle-point matrix [[A, Cm^T], [Cm, 0]], with A local_matrix's block and Cm the 20 x 729 primal constraints in the order of the coarse numbering: the value at each of the 8 corners, then the mean over the 7 inner nodes of each of the 12 edges. `coarse_basis`: block (a, b, c) is the constraint-by-node block of that same saddle-point inverse.
All inputs are finite; a program needn't handle non-finite values.
Results may differ from a plain program's by a relative error of at most 0.0014.
Values sent between devices are 32-bit elements; how exact they have to be, the bound alone decides.
No kernel may reach another device: no remote copies, remote signals or barrier semaphores. Data moves between devices by JAX's collectives and lax.ppermute only.
A program may use at most 128 MiB of HBM per device.

v0:
```python
import jax
import jax.numpy as jnp
from jax import lax
from jax.sharding import PartitionSpec as P

ITERS = 2


def with_halo(array, sides, width):
    for axis, dim in sides:
        size, length = (lax.axis_size(axis), array.shape[dim])
        up = [(i, (i + 1) % size) for i in range(size)]
        down = [(j, i) for i, j in up]
        last = lax.slice_in_dim(array, length - width, length, axis=dim)
        leading = lax.slice_in_dim(array, 0, width, axis=dim)
        before = lax.ppermute(last, axis, up)
        after = lax.ppermute(leading, axis, down)
        array = jnp.concatenate([before, array, after], axis=dim)
    return array


def matmul(left_side, right_side):
    return jnp.dot(
        left_side, right_side, precision=lax.Precision.HIGHEST, preferred_element_type=jnp.float32
    )


def coarse_ids(along_x, along_y, along_z, count_x, count_y, count_z):
    total = count_x * count_y * count_z

    def vertex(shift_x, shift_y, shift_z):
        return (
            (along_x + shift_x) % count_x * count_y + (along_y + shift_y) % count_y
        ) * count_z + (along_z + shift_z) % count_z

    listed = [vertex(sx, sy, sz) for sx in (0, 1) for sy in (0, 1) for sz in (0, 1)]
    listed += [total + vertex(0, sy, sz) for sy in (0, 1) for sz in (0, 1)]
    listed += [2 * total + vertex(sx, 0, sz) for sx in (0, 1) for sz in (0, 1)]
    listed += [3 * total + vertex(sx, sy, 0) for sx in (0, 1) for sy in (0, 1)]
    return jnp.stack(listed, axis=-1)


def node_weights(node_side):
    places = jnp.arange(node_side, dtype=jnp.int32)
    on_rim = ((places == 0) | (places == node_side - 1)).astype(jnp.int32)
    rims = on_rim[:, None, None] + on_rim[None, :, None] + on_rim[None, None, :]
    copies = (
        (1.0 + on_rim[:, None, None].astype(jnp.float32))
        * (1.0 + on_rim[None, :, None].astype(jnp.float32))
        * (1.0 + on_rim[None, None, :].astype(jnp.float32))
    )
    share = (1.0 / copies)[..., None]
    border = jnp.where(rims[..., None] > 0, share, jnp.zeros_like(share))
    return (share, border)


def fold_rim(padded, axis_dim):
    length = padded.shape[axis_dim]
    inside = lax.slice_in_dim(padded, 1, length - 1, axis=axis_dim)
    lowest = lax.slice_in_dim(padded, 0, 1, axis=axis_dim)
    highest = lax.slice_in_dim(padded, length - 1, length, axis=axis_dim)
    middle_shape = list(lowest.shape)
    middle_shape[axis_dim] = length - 4
    addend = jnp.concatenate(
        [lowest, jnp.zeros(middle_shape, padded.dtype), highest], axis=axis_dim
    )
    return inside + addend


def local(element_load, local_matrix, dirichlet_inverse, neumann_inverse, coarse_basis):
    highest_prec = lax.Precision.HIGHEST
    node_side = element_load.shape[0]
    rhs_count = element_load.shape[3]
    node_count = node_side**3
    inner_side = node_side - 2
    inner_count = inner_side**3
    primal = coarse_basis.shape[3]
    stiffness = local_matrix.reshape(node_count, node_count)
    interior_inverse = dirichlet_inverse.reshape(inner_count, inner_count)
    neumann = neumann_inverse.reshape(node_count, node_count)
    basis = coarse_basis.reshape(primal, node_count)
    stiff_cols = stiffness.reshape(node_count, node_side, node_side, node_side)[
        :, 1:-1, 1:-1, 1:-1
    ].reshape(node_count, inner_count)
    stiff_rows = stiffness.reshape(node_side, node_side, node_side, node_count)[
        1:-1, 1:-1, 1:-1
    ].reshape(inner_count, node_count)
    share, border = node_weights(node_side)
    count_x = lax.axis_size("gx")
    count_y = lax.axis_size("gy")
    count_z = lax.axis_size("gz")
    coarse_count = 4 * count_x * count_y * count_z
    own_ids = coarse_ids(
        lax.axis_index("gx"), lax.axis_index("gy"), lax.axis_index("gz"), count_x, count_y, count_z
    )
    columns = jnp.arange(coarse_count, dtype=jnp.int32)
    own_indicator = (own_ids[:, None] == columns[None, :]).astype(jnp.float32)
    coarse_local = matmul(basis, matmul(stiffness, basis.T))

    def piece_indicator(count_rows):
        linear = jnp.arange(count_rows, dtype=jnp.int32)
        piece_ids = coarse_ids(
            linear // (count_y * count_z),
            linear // count_z % count_y,
            linear % count_z,
            count_x,
            count_y,
            count_z,
        )
        return (piece_ids[:, :, None] == columns[None, None, :]).astype(jnp.float32)

    received = lax.all_gather(coarse_local[None], ("gx", "gy", "gz"), axis=0, tiled=True)
    indicator = piece_indicator(received.shape[0])
    partial_rows = jnp.einsum("zpm,zpq->zmq", indicator, received, precision=highest_prec)
    coarse_matrix = jnp.einsum("zmq,zqn->mn", partial_rows, indicator, precision=highest_prec)
    factor = jnp.linalg.cholesky(coarse_matrix)

    def coarse_rhs(primal_load):
        received = lax.all_gather(primal_load[None], ("gx", "gy", "gz"), axis=0, tiled=True)
        indicator = piece_indicator(received.shape[0])
        return jnp.einsum("zpm,zpk->mk", indicator, received, precision=highest_prec)

    def assemble(field):
        padded = with_halo(field, (("gx", 0),), 1)
        field = fold_rim(padded, 0)
        padded = with_halo(field, (("gy", 1),), 1)
        field = fold_rim(padded, 1)
        padded = with_halo(field, (("gz", 2),), 1)
        result_field = fold_rim(padded, 2)
        return result_field

    cube_shape = (node_side, node_side, node_side, rhs_count)

    def precondition(current):
        inner_part = current[1:-1, 1:-1, 1:-1].reshape(inner_count, rhs_count)
        start = matmul(interior_inverse, inner_part)
        spill = matmul(stiff_cols, start).reshape(cube_shape)
        first_residual = current - assemble(spill)
        weighted = (border * first_residual).reshape(node_count, rhs_count)
        local_part = matmul(neumann, weighted)
        primal_load = matmul(basis, weighted)
        coarse_values = jax.scipy.linalg.cho_solve((factor, True), coarse_rhs(primal_load))
        primal_values = matmul(own_indicator, coarse_values)
        combined = local_part + matmul(basis.T, primal_values)
        surface = assemble(border * combined.reshape(cube_shape))
        inner_new = start - matmul(
            interior_inverse, matmul(stiff_rows, surface.reshape(node_count, rhs_count))
        )
        padded_inner = jnp.pad(
            inner_new.reshape(inner_side, inner_side, inner_side, rhs_count),
            ((1, 1), (1, 1), (1, 1), (0, 0)),
        )
        return surface + padded_inner

    right_side = assemble(element_load)
    solution = jnp.zeros(cube_shape, jnp.float32)
    residual = right_side

    def precond_dot(left_field, right_field):
        return lax.psum(
            jnp.sum(left_field * right_field * share, axis=(0, 1, 2)), ("gx", "gy", "gz")
        )

    precond_now = precondition(residual)
    direction = precond_now
    energy = precond_dot(residual, precond_now)
    for iteration in range(ITERS):
        mapped = assemble(
            matmul(stiffness, direction.reshape(node_count, rhs_count)).reshape(cube_shape)
        )
        step_size = energy / lax.psum(
            jnp.sum(direction * mapped * share, axis=(0, 1, 2)), ("gx", "gy", "gz")
        )
        solution = solution + step_size * direction
        residual = residual - step_size * mapped
        if iteration + 1 < ITERS:
            precond_now = precondition(residual)
            energy_next = precond_dot(residual, precond_now)
            direction = precond_now + energy_next / energy * direction
            energy = energy_next
    return (solution, residual)


def solution(mesh):
    in_specs = (
        P("gx", "gy", "gz", None),
        P("gx", "gy", "gz", None, None),
        P("gx", "gy", "gz", None, None),
        P("gx", "gy", "gz", None, None),
        P("gx", "gy", "gz", None, None),
    )
    out_specs = (P("gx", "gy", "gz", None), P("gx", "gy", "gz", None))
    return jax.shard_map(local, mesh=mesh, in_specs=in_specs, out_specs=out_specs, check_vma=False)
```

profile of v0, /device:TPU:10, one launch (start us, length us, event | category | flops | bytes accessed | tf_op | source)
XLA Modules:
  0.0 518.0 jit_solution(8985004358485511838)
XLA Ops:
  4.9 3.7 fusion.4
  8.9 34.8 %all-gather.3 = f32[32,20,20]{2,1,0:T(8,128)S(1)} all-gather(f32[1,20,20]{2,1,0:T(8,128)S(1)} %copy.11), channel_id=2, replica_groups=mesh['gx'=4,'gy'=4,'gz'=2] {'gx','gy','gz'}, dimensions={0}, use_global_device_ids=true | all-gather | bytes 52800 | tf_op jit(solution)/shard_map/all_gather | solution.py:112
  46.4 3.1 collective-permute-start.3
  51.9 5.0 collective-permute-done.2
  58.9 5.0 copy.10
  63.9 3.7 reshape_reshape.6
  72.7 13.2 %cholesky.18 = f32[128,128]{1,0:T(8,128)} custom-call(f32[128,128]{1,0:T(8,128)} %fusion.80), custom_call_target="Cholesky" | custom-call | tf_op jit(solution)/shard_map/jit(cholesky)/cholesky | solution.py:116
  91.1 3.3 convolution_bitcast_fusion.1
  97.2 4.0 collective-permute-start.7
  119.0 11.3 %custom-call.9 = f32[1,128,128]{1,2,0:T(8,128)} custom-call(f32[1,128,128]{2,1,0:T(8,128)} %fusion.71), custom_call_target="InvertDiagBlocksLowerTriangular" | custom-call | tf_op jit(solution)/shard_map/jit(_cho_solve)/triangular_solve | solution.py:142
  136.7 3.7 fusion.8
  140.4 36.0 %all-gather.4 = f32[32,20,128]{2,1,0:T(8,128)S(1)} all-gather(f32[1,20,128]{2,1,0:T(8,128)S(1)} %convolution_bitcast_fusion.7), channel_id=3, replica_groups=mesh['gx'=4,'gy'=4,'gz'=2] {'gx','gy','gz'}, dimensions={0}, use_global_device_ids=true | all-gather | bytes 337920 | tf_op jit(solution)/shard_map/all_gather | solution.py:119
  182.5 4.5 collective-permute-start.13
  203.2 7.4 %reduce.6 = f32[729,729]{1,0:T(8,128)} reduce(f32[1,1,1,729,729]{4,2,3,1,0:T(1,128)S(1)} %copy-done, f32[]{:T(128)} %constant.929), dimensions={0,1,2}, to_apply=%param.8.reduce_sub_computation | reduce | bytes 4251532 | tf_op args[1]
  210.6 3.7 reshape_reshape.7
  254.8 3.0 collective-permute-done.21
  263.9 41.8 %all-reduce.2 = (f32[128]{0:T(128)}, f32[128]{0:T(128)}) all-reduce(f32[128]{0:T(128)} %get-tuple-element.4, f32[128]{0:T(128)} %get-tuple-element.3), channel_id=1, replica_groups=mesh['gx'=4,'gy'=4,'gz'=2] {'gx','gy','gz'}, use_global_device_ids=true, to_apply=%region_3.5 | all-reduce | flops 256 | bytes 2048 | tf_op jit(solution)/shard_map/psum | solution.py:160
  309.7 3.4 convolution_bitcast_fusion
  332.1 3.6 fusion.6
  336.1 37.3 %all-gather.5 = f32[32,20,128]{2,1,0:T(8,128)S(1)} all-gather(f32[1,20,128]{2,1,0:T(8,128)S(1)} %convolution_bitcast_fusion.6), channel_id=4, replica_groups=mesh['gx'=4,'gy'=4,'gz'=2] {'gx','gy','gz'}, dimensions={0}, use_global_device_ids=true | all-gather | bytes 337920 | tf_op jit(solution)/shard_map/all_gather | solution.py:119
  377.5 6.4 %collective-permute-start.31 = (f32[1,9,9,128]{3,2,1,0:T(8,128)S(1)}, f32[1,9,9,128]{3,2,1,0:T(8,128)S(1)}, u32[]{:S(2)}, u32[]{:S(2)}) collective-permute-start(f32[1,9,9,128]{3,2,1,0:T(8,128)S(1)} %get-tuple-element.16), channel_id=1, source_target_pairs={{8,0},{16,8},{24,16},{0,24},{9,1},{17,9},{25,17},{1,25},{10,2},{18... | collective-permute-start | bytes 124424 | tf_op jit(solution)/shard_map/ppermute | solution.py:17
  410.6 42.3 %psum.30 = f32[128]{0:T(128)S(1)} all-reduce(f32[128]{0:T(128)S(1)} %multiply_reduce_fusion.1), channel_id=1, replica_groups=mesh['gx'=4,'gy'=4,'gz'=2] {'gx','gy','gz'}, use_global_device_ids=true, to_apply=%region_7.9 | all-reduce | flops 128 | bytes 1024 | tf_op jit(solution)/shard_map/psum | solution.py:160
  460.6 2.9 collective-permute-start.36
  473.2 43.2 %psum.31 = f32[128]{0:T(128)S(1)} all-reduce(f32[128]{0:T(128)S(1)} %multiply_reduce_fusion), channel_id=1, replica_groups=mesh['gx'=4,'gy'=4,'gz'=2] {'gx','gy','gz'}, use_global_device_ids=true, to_apply=%region_9.11 | all-reduce | flops 128 | bytes 1024 | tf_op jit(solution)/shard_map/psum | solution.py:171
  (317 shorter events, 189.9 us)
Async XLA Ops:
  1.6 44.6 %collective-permute-start.1 = (f32[1,9,9,128]{3,2,1,0:T(8,128)S(1)}, f32[1,9,9,128]{3,2,1,0:T(8,128)S(1)}, u32[]{:S(2)}, u32[]{:S(2)}) collective-permute-start(f32[1,9,9,128]{3,2,1,0:T(8,128)S(1)} %get-tuple-element.40), channel_id=1, source_target_pairs={{8,0},{16,8},{24,16},{0,24},{9,1},{17,9},{25,17},{1,25},{10,2},{18... | collective-permute-start | bytes 124424 | tf_op jit(solution)/shard_map/ppermute | solution.py:17
  2.2 44.1 %collective-permute-start = (f32[1,9,9,128]{3,2,1,0:T(8,128)S(1)}, f32[1,9,9,128]{3,2,1,0:T(8,128)S(1)}, u32[]{:S(2)}, u32[]{:S(2)}) collective-permute-start(f32[1,9,9,128]{3,2,1,0:T(8,128)S(1)} %get-tuple-element.39), channel_id=1, source_target_pairs={{0,8},{8,16},{16,24},{24,0},{1,9},{9,17},{17,25},{25,1},{2,10},{10... | collective-permute-start | bytes 124424 | tf_op jit(solution)/shard_map/ppermute | solution.py:16
  46.4 5.5 %collective-permute-start.3 = (f32[9,1,9,128]{3,2,1,0:T(8,128)S(1)}, f32[9,1,9,128]{3,2,1,0:T(8,128)S(1)}, u32[]{:S(2)}, u32[]{:S(2)}) collective-permute-start(f32[9,1,9,128]{3,2,1,0:T(8,128)S(1)} %get-tuple-element.38), channel_id=1, source_target_pairs={{2,0},{4,2},{6,4},{0,6},{3,1},{5,3},{7,5},{1,7},{10,8},{12,10},{14... | collective-permute-start | bytes 124424 | tf_op jit(solution)/shard_map/ppermute | solution.py:17
  49.5 7.3 %collective-permute-start.2 = (f32[9,1,9,128]{3,2,1,0:T(8,128)S(1)}, f32[9,1,9,128]{3,2,1,0:T(8,128)S(1)}, u32[]{:S(2)}, u32[]{:S(2)}) collective-permute-start(f32[9,1,9,128]{3,2,1,0:T(8,128)S(1)} %get-tuple-element.37), channel_id=1, source_target_pairs={{0,2},{2,4},{4,6},{6,0},{1,3},{3,5},{5,7},{7,1},{8,10},{10,12},{12... | collective-permute-start | bytes 124424 | tf_op jit(solution)/shard_map/ppermute | solution.py:16
  57.7 28.2 %collective-permute-start.5 = (f32[9,9,1,128]{3,2,1,0:T(1,128)}, f32[9,9,1,128]{3,2,1,0:T(1,128)S(1)}, u32[]{:S(2)}, u32[]{:S(2)}) collective-permute-start(f32[9,9,1,128]{3,2,1,0:T(1,128)} %get-tuple-element.36), channel_id=1, source_target_pairs={{1,0},{0,1},{3,2},{2,3},{5,4},{4,5},{7,6},{6,7},{9,8},{8,9},{11,10... | collective-permute-start | bytes 124424 | tf_op jit(solution)/shard_map/ppermute | solution.py:17
  57.7 28.2 %collective-permute-start.4 = (f32[9,9,1,128]{3,2,1,0:T(1,128)}, f32[9,9,1,128]{3,2,1,0:T(1,128)}, u32[]{:S(2)}, u32[]{:S(2)}) collective-permute-start(f32[9,9,1,128]{3,2,1,0:T(1,128)} %get-tuple-element.35), channel_id=1, source_target_pairs={{0,1},{1,0},{2,3},{3,2},{4,5},{5,4},{6,7},{7,6},{8,9},{9,8},{10,11... | collective-permute-start | bytes 124424 | tf_op jit(solution)/shard_map/ppermute | solution.py:16
  97.2 8.7 %collective-permute-start.7 = (f32[1,9,9,128]{3,2,1,0:T(8,128)}, f32[1,9,9,128]{3,2,1,0:T(8,128)}, u32[]{:S(2)}, u32[]{:S(2)}) collective-permute-start(f32[1,9,9,128]{3,2,1,0:T(8,128)} %slice.187), channel_id=1, source_target_pairs={{8,0},{16,8},{24,16},{0,24},{9,1},{17,9},{25,17},{1,25},{10,2},{18... | collective-permute-start | bytes 124424 | tf_op jit(solution)/shard_map/ppermute | solution.py:17
  102.7 4.7 collective-permute-start.6
  108.6 5.1 collective-permute-start.9
  117.2 13.7 %collective-permute-start.11 = (f32[9,9,1,128]{3,2,1,0:T(1,128)}, f32[9,9,1,128]{3,2,1,0:T(1,128)}, u32[]{:S(2)}, u32[]{:S(2)}) collective-permute-start(f32[9,9,1,128]{3,2,1,0:T(1,128)} %get-tuple-element.32), channel_id=1, source_target_pairs={{1,0},{0,1},{3,2},{2,3},{5,4},{4,5},{7,6},{6,7},{9,8},{8,9},{11,10... | collective-permute-start | bytes 124424 | tf_op jit(solution)/shard_map/ppermute | solution.py:17
  117.2 13.7 %collective-permute-start.10 = (f32[9,9,1,128]{3,2,1,0:T(1,128)}, f32[9,9,1,128]{3,2,1,0:T(1,128)}, u32[]{:S(2)}, u32[]{:S(2)}) collective-permute-start(f32[9,9,1,128]{3,2,1,0:T(1,128)} %get-tuple-element.31), channel_id=1, source_target_pairs={{0,1},{1,0},{2,3},{3,2},{4,5},{5,4},{6,7},{7,6},{8,9},{9,8},{10,11... | collective-permute-start | bytes 124424 | tf_op jit(solution)/shard_map/ppermute | solution.py:16
  182.5 7.6 %collective-permute-start.13 = (f32[1,9,9,128]{3,2,1,0:T(8,128)S(1)}, f32[1,9,9,128]{3,2,1,0:T(8,128)S(1)}, u32[]{:S(2)}, u32[]{:S(2)}) collective-permute-start(f32[1,9,9,128]{3,2,1,0:T(8,128)S(1)} %get-tuple-element.30), channel_id=1, source_target_pairs={{8,0},{16,8},{24,16},{0,24},{9,1},{17,9},{25,17},{1,25},{10,2},{18... | collective-permute-start | bytes 124424 | tf_op jit(solution)/shard_map/ppermute | solution.py:17
  202.0 21.0 %collective-permute-start.17 = (f32[9,9,1,128]{3,2,1,0:T(1,128)}, f32[9,9,1,128]{3,2,1,0:T(1,128)}, u32[]{:S(2)}, u32[]{:S(2)}) collective-permute-start(f32[9,9,1,128]{3,2,1,0:T(1,128)} %get-tuple-element.26), channel_id=1, source_target_pairs={{1,0},{0,1},{3,2},{2,3},{5,4},{4,5},{7,6},{6,7},{9,8},{8,9},{11,10... | collective-permute-start | bytes 124424 | tf_op jit(solution)/shard_map/ppermute | solution.py:17
  202.0 21.0 %collective-permute-start.16 = (f32[9,9,1,128]{3,2,1,0:T(1,128)}, f32[9,9,1,128]{3,2,1,0:T(1,128)}, u32[]{:S(2)}, u32[]{:S(2)}) collective-permute-start(f32[9,9,1,128]{3,2,1,0:T(1,128)} %get-tuple-element.25), channel_id=1, source_target_pairs={{0,1},{1,0},{2,3},{3,2},{4,5},{5,4},{6,7},{7,6},{8,9},{9,8},{10,11... | collective-permute-start | bytes 124424 | tf_op jit(solution)/shard_map/ppermute | solution.py:16
  242.3 6.6 %collective-permute-start.19 = (f32[1,9,9,128]{3,2,1,0:T(8,128)}, f32[1,9,9,128]{3,2,1,0:T(8,128)}, u32[]{:S(2)}, u32[]{:S(2)}) collective-permute-start(f32[1,9,9,128]{3,2,1,0:T(8,128)} %slice.202), channel_id=1, source_target_pairs={{8,0},{16,8},{24,16},{0,24},{9,1},{17,9},{25,17},{1,25},{10,2},{18... | collective-permute-start | bytes 124424 | tf_op jit(solution)/shard_map/ppermute | solution.py:17
  246.4 5.1 collective-permute-start.18
  252.7 5.1 collective-permute-start.21
  313.8 5.6 %collective-permute-start.25 = (f32[1,9,9,128]{3,2,1,0:T(8,128)}, f32[1,9,9,128]{3,2,1,0:T(8,128)}, u32[]{:S(2)}, u32[]{:S(2)}) collective-permute-start(f32[1,9,9,128]{3,2,1,0:T(8,128)} %slice.211), channel_id=1, source_target_pairs={{8,0},{16,8},{24,16},{0,24},{9,1},{17,9},{25,17},{1,25},{10,2},{18... | collective-permute-start | bytes 124424 | tf_op jit(solution)/shard_map/ppermute | solution.py:17
  314.5 5.5 %collective-permute-start.24 = (f32[1,9,9,128]{3,2,1,0:T(8,128)}, f32[1,9,9,128]{3,2,1,0:T(8,128)}, u32[]{:S(2)}, u32[]{:S(2)}) collective-permute-start(f32[1,9,9,128]{3,2,1,0:T(8,128)} %slice.209), channel_id=1, source_target_pairs={{0,8},{8,16},{16,24},{24,0},{1,9},{9,17},{17,25},{25,1},{2,10},{10... | collective-permute-start | bytes 124424 | tf_op jit(solution)/shard_map/ppermute | solution.py:16
  377.5 9.2 %collective-permute-start.31 = (f32[1,9,9,128]{3,2,1,0:T(8,128)S(1)}, f32[1,9,9,128]{3,2,1,0:T(8,128)S(1)}, u32[]{:S(2)}, u32[]{:S(2)}) collective-permute-start(f32[1,9,9,128]{3,2,1,0:T(8,128)S(1)} %get-tuple-element.16), channel_id=1, source_target_pairs={{8,0},{16,8},{24,16},{0,24},{9,1},{17,9},{25,17},{1,25},{10,2},{18... | collective-permute-start | bytes 124424 | tf_op jit(solution)/shard_map/ppermute | solution.py:17
  389.8 5.1 collective-permute-start.32
  460.5 5.3 %collective-permute-start.37 = (f32[1,9,9,128]{3,2,1,0:T(8,128)S(1)}, f32[1,9,9,128]{3,2,1,0:T(8,128)S(1)}, u32[]{:S(2)}, u32[]{:S(2)}) collective-permute-start(f32[1,9,9,128]{3,2,1,0:T(8,128)S(1)} %slice.225), channel_id=1, source_target_pairs={{8,0},{16,8},{24,16},{0,24},{9,1},{17,9},{25,17},{1,25},{10,2},{18... | collective-permute-start | bytes 124424 | tf_op jit(solution)/shard_map/ppermute | solution.py:17
  460.6 5.3 %collective-permute-start.36 = (f32[1,9,9,128]{3,2,1,0:T(8,128)S(1)}, f32[1,9,9,128]{3,2,1,0:T(8,128)S(1)}, u32[]{:S(2)}, u32[]{:S(2)}) collective-permute-start(f32[1,9,9,128]{3,2,1,0:T(8,128)S(1)} %slice.223), channel_id=1, source_target_pairs={{0,8},{8,16},{16,24},{24,0},{1,9},{9,17},{17,25},{25,1},{2,10},{10... | collective-permute-start | bytes 124424 | tf_op jit(solution)/shard_map/ppermute | solution.py:16
  466.2 5.0 collective-permute-start.38
  (70 other events, 876.4 us)
where the time goes:
time: 524 us; the launch traced here: 518 us
  blocking collectives  235 us (45%)
  other arithmetic  73.6 us (14%)
  local copies, waits for them, and re-layouts  71.8 us (14%)
  starting transfers between devices  47.7 us (9%)
  waiting for transfers between devices  45 us (9%)
  matrix products  42.8 us (8%)
    psum x2, blocking collectives, precond_dot(): lax.psum(jnp.sum(left_field * right_field * share, axis=(0, 1, 2)), ('gx'...  84.1 us
    all_gather x2, blocking collectives, coarse_rhs(): lax.all_gather(primal_load[None], ('gx', 'gy', 'gz'), axis=0, tiled=True)  73.3 us
    psum x1, blocking collectives, local(): lax.psum(jnp.sum(direction * mapped * share, axis=(0, 1, 2)), ('gx', 'gy'...  43.2 us
    dot_general x20, matrix products, matmul(): jnp.dot(left_side, right_side, precision=lax.Precision.HIGHEST, preferred...  39.7 us
    all_gather x1, blocking collectives, local(): lax.all_gather(coarse_local[None], ('gx', 'gy', 'gz'), axis=0, tiled=True)  34.8 us
    ppermute x21, starting transfers between devices, with_halo(): after = lax.ppermute(leading, axis, down)  27.8 us
    ppermute x21, waiting for transfers between devices, with_halo(): after = lax.ppermute(leading, axis, down)  25.5 us
    ppermute x21, starting transfers between devices, with_halo(): before = lax.ppermute(last, axis, up)  19.9 us
  transfers between devices with their start and end apart: 42, of which 30 were waited for; matrix products, arithmetic and copies ran while one was open for 16% of the time, Pallas kernels for 0%

commit v1 on v0

--- a/solution.py
+++ b/solution.py
@@ -157,8 +157,11 @@
     residual = right_side
 
     def precond_dot(left_field, right_field):
-        return lax.psum(
-            jnp.sum(left_field * right_field * share, axis=(0, 1, 2)), ("gx", "gy", "gz")
+        return jnp.sum(
+            lax.all_gather(
+                jnp.sum(left_field * right_field * share, axis=(0, 1, 2)), ("gx", "gy", "gz")
+            ),
+            axis=0,
         )
 
     precond_now = precondition(residual)

time: 524 us -> 561 us (1.071)
  blocking collectives: 235 us -> 266 us
    psum x2 -> x0, blocking collectives: 84.1 us -> none  [precond_dot(): lax.psum(jnp.sum(left_field * right_field * share, axis=(0, 1, 2)), ('gx'...]
    all_gather x0 -> x2, blocking collectives: none -> 72.1 us  [precond_dot(): lax.all_gather(jnp.sum(left_field * right_field * share, axis=(0, 1, 2)),...]
    psum x1 -> x2, blocking collectives: 43.2 us -> 85.8 us  [local(): lax.psum(jnp.sum(direction * mapped * share, axis=(0, 1, 2)), ('gx', 'gy'...]
    ppermute x21, starting transfers between devices: 27.8 us -> 35 us  [with_halo(): after = lax.ppermute(leading, axis, down)]
  transfers between devices with their start and end apart: 42 -> 42, of which waited for: 30 -> 30; matrix products, arithmetic and copies ran while one was open for 16% -> 15% of each run, Pallas kernels for 0% -> 0%
where the time goes in v1:
time: 561 us; the launch traced here: 555 us
  blocking collectives  266 us (47%)
  other arithmetic  74.9 us (13%)
  local copies, waits for them, and re-layouts  71.8 us (13%)
  starting transfers between devices  50.9 us (9%)
  waiting for transfers between devices  47.1 us (8%)
  matrix products  42.8 us (8%)
    psum x2, blocking collectives, local(): lax.psum(jnp.sum(direction * mapped * share, axis=(0, 1, 2)), ('gx', 'gy'...  85.8 us
    all_gather x2, blocking collectives, coarse_rhs(): lax.all_gather(primal_load[None], ('gx', 'gy', 'gz'), axis=0, tiled=True)  73.4 us
    all_gather x2, blocking collectives, precond_dot(): lax.all_gather(jnp.sum(left_field * right_field * share, axis=(0, 1, 2)),...  72.1 us
    dot_general x20, matrix products, matmul(): jnp.dot(left_side, right_side, precision=lax.Precision.HIGHEST, preferred...  39.7 us
    ppermute x21, starting transfers between devices, with_halo(): after = lax.ppermute(leading, axis, down)  35 us
    all_gather x1, blocking collectives, local(): lax.all_gather(coarse_local[None], ('gx', 'gy', 'gz'), axis=0, tiled=True)  34.8 us
    ppermute x21, waiting for transfers between devices, with_halo(): after = lax.ppermute(leading, axis, down)  26.7 us
    ppermute x21, waiting for transfers between devices, with_halo(): before = lax.ppermute(last, axis, up)  20.4 us
  transfers between devices with their start and end apart: 42, of which 30 were waited for; matrix products, arithmetic and copies ran while one was open for 15% of the time, Pallas kernels for 0%

profile of v1, /device:TPU:10, one launch (start us, length us, event | category | flops | bytes accessed | tf_op | source)
XLA Modules:
  0.0 555.2 jit_solution(17163727876763686867)
XLA Ops:
  4.9 3.7 fusion.4
  8.9 34.8 %all-gather.5 = f32[32,20,20]{2,1,0:T(8,128)S(1)} all-gather(f32[1,20,20]{2,1,0:T(8,128)S(1)} %copy.11), channel_id=2, replica_groups=mesh['gx'=4,'gy'=4,'gz'=2] {'gx','gy','gz'}, dimensions={0}, use_global_device_ids=true | all-gather | bytes 52800 | tf_op jit(solution)/shard_map/all_gather | solution.py:112
  46.4 3.1 collective-permute-start.3
  51.9 5.0 collective-permute-done.2
  58.9 5.0 copy.10
  64.0 3.7 reshape_reshape.6
  72.7 13.2 %cholesky.18 = f32[128,128]{1,0:T(8,128)} custom-call(f32[128,128]{1,0:T(8,128)} %fusion.80), custom_call_target="Cholesky" | custom-call | tf_op jit(solution)/shard_map/jit(cholesky)/cholesky | solution.py:116
  91.1 3.3 convolution_bitcast_fusion.1
  97.2 4.0 collective-permute-start.7
  119.0 11.3 %custom-call.9 = f32[1,128,128]{1,2,0:T(8,128)} custom-call(f32[1,128,128]{2,1,0:T(8,128)} %fusion.71), custom_call_target="InvertDiagBlocksLowerTriangular" | custom-call | tf_op jit(solution)/shard_map/jit(_cho_solve)/triangular_solve | solution.py:142
  136.8 3.7 fusion.8
  140.5 36.0 %all-gather.6 = f32[32,20,128]{2,1,0:T(8,128)S(1)} all-gather(f32[1,20,128]{2,1,0:T(8,128)S(1)} %convolution_bitcast_fusion.7), channel_id=3, replica_groups=mesh['gx'=4,'gy'=4,'gz'=2] {'gx','gy','gz'}, dimensions={0}, use_global_device_ids=true | all-gather | bytes 337920 | tf_op jit(solution)/shard_map/all_gather | solution.py:119
  182.6 4.5 collective-permute-start.13
  203.3 7.4 %reduce.8 = f32[729,729]{1,0:T(8,128)} reduce(f32[1,1,1,729,729]{4,2,3,1,0:T(1,128)S(1)} %copy-done, f32[]{:T(128)} %constant.929), dimensions={0,1,2}, to_apply=%param.8.reduce_sub_computation | reduce | bytes 4251532 | tf_op args[1]
  210.7 3.7 reshape_reshape.7
  263.9 36.2 %all-gather.7 = f32[32,1,128]{2,1,0:T(1,128)} all-gather(f32[1,1,128]{2,1,0:T(1,128)S(1)} %bitcast.143), channel_id=4, replica_groups=mesh['gx'=4,'gy'=4,'gz'=2] {'gx','gy','gz'}, dimensions={0}, use_global_device_ids=true | all-gather | bytes 16896 | tf_op jit(solution)/shard_map/all_gather | solution.py:161
  301.5 43.6 %psum.14 = f32[128]{0:T(128)} all-reduce(f32[128]{0:T(128)} %get-tuple-element.3), channel_id=1, replica_groups=mesh['gx'=4,'gy'=4,'gz'=2] {'gx','gy','gz'}, use_global_device_ids=true, to_apply=%region_5.7 | all-reduce | flops 128 | bytes 1024 | tf_op jit(solution)/shard_map/psum | solution.py:174
  349.0 3.3 convolution_bitcast_fusion
  372.8 3.6 fusion.6
  376.8 37.3 %all-gather.8 = f32[32,20,128]{2,1,0:T(8,128)S(1)} all-gather(f32[1,20,128]{2,1,0:T(8,128)S(1)} %convolution_bitcast_fusion.6), channel_id=5, replica_groups=mesh['gx'=4,'gy'=4,'gz'=2] {'gx','gy','gz'}, dimensions={0}, use_global_device_ids=true | all-gather | bytes 337920 | tf_op jit(solution)/shard_map/all_gather | solution.py:119
  418.3 6.0 %collective-permute-start.31 = (f32[1,9,9,128]{3,2,1,0:T(8,128)S(1)}, f32[1,9,9,128]{3,2,1,0:T(8,128)S(1)}, u32[]{:S(2)}, u32[]{:S(2)}) collective-permute-start(f32[1,9,9,128]{3,2,1,0:T(8,128)S(1)} %get-tuple-element.14), channel_id=1, source_target_pairs={{8,0},{16,8},{24,16},{0,24},{9,1},{17,9},{25,17},{1,25},{10,2},{18... | collective-permute-start | bytes 124424 | tf_op jit(solution)/shard_map/ppermute | solution.py:17
  450.9 35.8 %all-gather.9 = f32[32,1,128]{2,1,0:T(1,128)S(1)} all-gather(f32[1,1,128]{2,1,0:T(1,128)S(1)} %bitcast.142), channel_id=6, replica_groups=mesh['gx'=4,'gy'=4,'gz'=2] {'gx','gy','gz'}, dimensions={0}, use_global_device_ids=true | all-gather | bytes 16896 | tf_op jit(solution)/shard_map/all_gather | solution.py:161
  494.5 4.8 collective-permute-start.37
  511.4 42.2 %psum.15 = f32[128]{0:T(128)S(1)} all-reduce(f32[128]{0:T(128)S(1)} %multiply_reduce_fusion), channel_id=1, replica_groups=mesh['gx'=4,'gy'=4,'gz'=2] {'gx','gy','gz'}, use_global_device_ids=true, to_apply=%region_9.11 | all-reduce | flops 128 | bytes 1024 | tf_op jit(solution)/shard_map/psum | solution.py:174
  (320 shorter events, 198.0 us)
Async XLA Ops:
  1.6 44.6 %collective-permute-start.1 = (f32[1,9,9,128]{3,2,1,0:T(8,128)S(1)}, f32[1,9,9,128]{3,2,1,0:T(8,128)S(1)}, u32[]{:S(2)}, u32[]{:S(2)}) collective-permute-start(f32[1,9,9,128]{3,2,1,0:T(8,128)S(1)} %get-tuple-element.38), channel_id=1, source_target_pairs={{8,0},{16,8},{24,16},{0,24},{9,1},{17,9},{25,17},{1,25},{10,2},{18... | collective-permute-start | bytes 124424 | tf_op jit(solution)/shard_map/ppermute | solution.py:17
  2.2 44.1 %collective-permute-start = (f32[1,9,9,128]{3,2,1,0:T(8,128)S(1)}, f32[1,9,9,128]{3,2,1,0:T(8,128)S(1)}, u32[]{:S(2)}, u32[]{:S(2)}) collective-permute-start(f32[1,9,9,128]{3,2,1,0:T(8,128)S(1)} %get-tuple-element.37), channel_id=1, source_target_pairs={{0,8},{8,16},{16,24},{24,0},{1,9},{9,17},{17,25},{25,1},{2,10},{10... | collective-permute-start | bytes 124424 | tf_op jit(solution)/shard_map/ppermute | solution.py:16
  46.4 5.5 collective-permute-start.3
  49.5 7.3 %collective-permute-start.2 = (f32[9,1,9,128]{3,2,1,0:T(8,128)S(1)}, f32[9,1,9,128]{3,2,1,0:T(8,128)S(1)}, u32[]{:S(2)}, u32[]{:S(2)}) collective-permute-start(f32[9,1,9,128]{3,2,1,0:T(8,128)S(1)} %get-tuple-element.35), channel_id=1, source_target_pairs={{0,2},{2,4},{4,6},{6,0},{1,3},{3,5},{5,7},{7,1},{8,10},{10,12},{12... | collective-permute-start | bytes 124424 | tf_op jit(solution)/shard_map/ppermute | solution.py:16
  57.7 28.2 %collective-permute-start.5 = (f32[9,9,1,128]{3,2,1,0:T(1,128)}, f32[9,9,1,128]{3,2,1,0:T(1,128)S(1)}, u32[]{:S(2)}, u32[]{:S(2)}) collective-permute-start(f32[9,9,1,128]{3,2,1,0:T(1,128)} %get-tuple-element.34), channel_id=1, source_target_pairs={{1,0},{0,1},{3,2},{2,3},{5,4},{4,5},{7,6},{6,7},{9,8},{8,9},{11,10... | collective-permute-start | bytes 124424 | tf_op jit(solution)/shard_map/ppermute | solution.py:17
  57.7 28.2 %collective-permute-start.4 = (f32[9,9,1,128]{3,2,1,0:T(1,128)}, f32[9,9,1,128]{3,2,1,0:T(1,128)}, u32[]{:S(2)}, u32[]{:S(2)}) collective-permute-start(f32[9,9,1,128]{3,2,1,0:T(1,128)} %get-tuple-element.33), channel_id=1, source_target_pairs={{0,1},{1,0},{2,3},{3,2},{4,5},{5,4},{6,7},{7,6},{8,9},{9,8},{10,11... | collective-permute-start | bytes 124424 | tf_op jit(solution)/shard_map/ppermute | solution.py:16
  97.2 8.7 %collective-permute-start.7 = (f32[1,9,9,128]{3,2,1,0:T(8,128)}, f32[1,9,9,128]{3,2,1,0:T(8,128)}, u32[]{:S(2)}, u32[]{:S(2)}) collective-permute-start(f32[1,9,9,128]{3,2,1,0:T(8,128)} %slice.187), channel_id=1, source_target_pairs={{8,0},{16,8},{24,16},{0,24},{9,1},{17,9},{25,17},{1,25},{10,2},{18... | collective-permute-start | bytes 124424 | tf_op jit(solution)/shard_map/ppermute | solution.py:17
  102.7 4.7 collective-permute-start.6
  108.6 5.1 collective-permute-start.9
  117.2 13.8 %collective-permute-start.11 = (f32[9,9,1,128]{3,2,1,0:T(1,128)}, f32[9,9,1,128]{3,2,1,0:T(1,128)}, u32[]{:S(2)}, u32[]{:S(2)}) collective-permute-start(f32[9,9,1,128]{3,2,1,0:T(1,128)} %get-tuple-element.30), channel_id=1, source_target_pairs={{1,0},{0,1},{3,2},{2,3},{5,4},{4,5},{7,6},{6,7},{9,8},{8,9},{11,10... | collective-permute-start | bytes 124424 | tf_op jit(solution)/shard_map/ppermute | solution.py:17
  117.2 13.8 %collective-permute-start.10 = (f32[9,9,1,128]{3,2,1,0:T(1,128)}, f32[9,9,1,128]{3,2,1,0:T(1,128)}, u32[]{:S(2)}, u32[]{:S(2)}) collective-permute-start(f32[9,9,1,128]{3,2,1,0:T(1,128)} %get-tuple-element.29), channel_id=1, source_target_pairs={{0,1},{1,0},{2,3},{3,2},{4,5},{5,4},{6,7},{7,6},{8,9},{9,8},{10,11... | collective-permute-start | bytes 124424 | tf_op jit(solution)/shard_map/ppermute | solution.py:16
  182.6 7.6 %collective-permute-start.13 = (f32[1,9,9,128]{3,2,1,0:T(8,128)S(1)}, f32[1,9,9,128]{3,2,1,0:T(8,128)S(1)}, u32[]{:S(2)}, u32[]{:S(2)}) collective-permute-start(f32[1,9,9,128]{3,2,1,0:T(8,128)S(1)} %get-tuple-element.28), channel_id=1, source_target_pairs={{8,0},{16,8},{24,16},{0,24},{9,1},{17,9},{25,17},{1,25},{10,2},{18... | collective-permute-start | bytes 124424 | tf_op jit(solution)/shard_map/ppermute | solution.py:17
  202.1 21.0 %collective-permute-start.17 = (f32[9,9,1,128]{3,2,1,0:T(1,128)}, f32[9,9,1,128]{3,2,1,0:T(1,128)}, u32[]{:S(2)}, u32[]{:S(2)}) collective-permute-start(f32[9,9,1,128]{3,2,1,0:T(1,128)} %get-tuple-element.24), channel_id=1, source_target_pairs={{1,0},{0,1},{3,2},{2,3},{5,4},{4,5},{7,6},{6,7},{9,8},{8,9},{11,10... | collective-permute-start | bytes 124424 | tf_op jit(solution)/shard_map/ppermute | solution.py:17
  202.1 21.0 %collective-permute-start.16 = (f32[9,9,1,128]{3,2,1,0:T(1,128)}, f32[9,9,1,128]{3,2,1,0:T(1,128)}, u32[]{:S(2)}, u32[]{:S(2)}) collective-permute-start(f32[9,9,1,128]{3,2,1,0:T(1,128)} %get-tuple-element.23), channel_id=1, source_target_pairs={{0,1},{1,0},{2,3},{3,2},{4,5},{5,4},{6,7},{7,6},{8,9},{9,8},{10,11... | collective-permute-start | bytes 124424 | tf_op jit(solution)/shard_map/ppermute | solution.py:16
  242.4 6.7 %collective-permute-start.19 = (f32[1,9,9,128]{3,2,1,0:T(8,128)}, f32[1,9,9,128]{3,2,1,0:T(8,128)}, u32[]{:S(2)}, u32[]{:S(2)}) collective-permute-start(f32[1,9,9,128]{3,2,1,0:T(8,128)} %slice.202), channel_id=1, source_target_pairs={{8,0},{16,8},{24,16},{0,24},{9,1},{17,9},{25,17},{1,25},{10,2},{18... | collective-permute-start | bytes 124424 | tf_op jit(solution)/shard_map/ppermute | solution.py:17
  246.5 5.1 collective-permute-start.18
  252.8 5.1 collective-permute-start.21
  353.1 5.6 %collective-permute-start.25 = (f32[1,9,9,128]{3,2,1,0:T(8,128)}, f32[1,9,9,128]{3,2,1,0:T(8,128)}, u32[]{:S(2)}, u32[]{:S(2)}) collective-permute-start(f32[1,9,9,128]{3,2,1,0:T(8,128)} %slice.211), channel_id=1, source_target_pairs={{8,0},{16,8},{24,16},{0,24},{9,1},{17,9},{25,17},{1,25},{10,2},{18... | collective-permute-start | bytes 124424 | tf_op jit(solution)/shard_map/ppermute | solution.py:17
  353.8 5.2 collective-permute-start.24
  360.2 5.1 collective-permute-start.27
  362.1 4.7 collective-permute-start.26
  418.3 9.7 %collective-permute-start.31 = (f32[1,9,9,128]{3,2,1,0:T(8,128)S(1)}, f32[1,9,9,128]{3,2,1,0:T(8,128)S(1)}, u32[]{:S(2)}, u32[]{:S(2)}) collective-permute-start(f32[1,9,9,128]{3,2,1,0:T(8,128)S(1)} %get-tuple-element.14), channel_id=1, source_target_pairs={{8,0},{16,8},{24,16},{0,24},{9,1},{17,9},{25,17},{1,25},{10,2},{18... | collective-permute-start | bytes 124424 | tf_op jit(solution)/shard_map/ppermute | solution.py:17
  430.2 5.1 collective-permute-start.32
  494.5 8.4 %collective-permute-start.37 = (f32[1,9,9,128]{3,2,1,0:T(8,128)S(1)}, f32[1,9,9,128]{3,2,1,0:T(8,128)S(1)}, u32[]{:S(2)}, u32[]{:S(2)}) collective-permute-start(f32[1,9,9,128]{3,2,1,0:T(8,128)S(1)} %slice.225), channel_id=1, source_target_pairs={{8,0},{16,8},{24,16},{0,24},{9,1},{17,9},{25,17},{1,25},{10,2},{18... | collective-permute-start | bytes 124424 | tf_op jit(solution)/shard_map/ppermute | solution.py:17
  (70 other events, 870.3 us)
